TPU v7x, 32 devices: a whole 2x2x4 slice. The times are simulated.
32 devices in a mesh: farcp: 4 (over z), nearcp: 4 (over y, x), tp: 2 (over core).
Axes of the slice: x: 2, y: 2, z: 4, core: 2. Of those that a mesh axis runs over, the one named last changes fastest.
Arguments:
- raw_keys: bfloat16 [16, 8192, 8, 128], P(None, ('farcp', 'nearcp'), 'tp'), may hold values from -6 to 6
- raw_values: bfloat16 [16, 8192, 8, 128], P(None, ('farcp', 'nearcp'), 'tp'), may hold values from -6 to 6
- turn_angle: float32 [8192, 64], replicated, may hold values from -3.140625 to 3.140625
Outputs:
- stored_keys: bfloat16 [16, 8192, 8, 128], P(('farcp', 'nearcp'), None, 'tp')
- stored_values: bfloat16 [16, 8192, 8, 128], P(('farcp', 'nearcp'), None, 'tp')
- key_scale: float32 [16, 8, 128], P(('farcp', 'nearcp'), 'tp')
All inputs are finite; a program needn't handle non-finite values. Where the computation divides by a largest or mean magnitude, that divisor is 1e-20 or more.
Results may differ from a plain program's by a relative error of at most 0.001.
Values may be sent and summed in bfloat16 or wider, within the bound.
No kernel may reach another device: no remote copies, remote signals or barrier semaphores. Data moves between devices by JAX's collectives and lax.ppermute only.
A program may use at most 128 MiB of HBM per device.

v0:
```python
import jax
import jax.numpy as jnp
from jax import lax
from jax.sharding import PartitionSpec as P


def turn_pairs(vectors, angle):
    half = vectors.shape[-1] // 2
    cosine, sine = (jnp.cos(angle)[None, :, None, :], jnp.sin(angle)[None, :, None, :])
    first, second = (vectors[..., :half], vectors[..., half:])
    return jnp.concatenate(
        [first * cosine - second * sine, second * cosine + first * sine], axis=-1
    )


def ready_to_store(plain_keys, angle):
    wide_keys = plain_keys.astype(jnp.float32)
    return turn_pairs(wide_keys, angle)


def body(raw_keys, raw_values, turn_angle):
    moved_keys, stored_values = (
        lax.all_to_all(raw_keys, ("farcp", "nearcp"), split_axis=0, concat_axis=1, tiled=True),
        lax.all_to_all(raw_values, ("farcp", "nearcp"), split_axis=0, concat_axis=1, tiled=True),
    )
    turned_keys = ready_to_store(moved_keys, turn_angle)
    key_scale = jnp.max(jnp.abs(turned_keys), axis=1)
    narrow_keys = (turned_keys / key_scale[:, None]).astype(jnp.bfloat16)
    return (narrow_keys, stored_values, key_scale)


def solution(mesh):
    placed = (
        P(None, ("farcp", "nearcp"), "tp", None),
        P(None, ("farcp", "nearcp"), "tp", None),
        P(),
    )
    return jax.shard_map(
        body,
        mesh=mesh,
        in_specs=placed,
        out_specs=(
            P(("farcp", "nearcp"), None, "tp", None),
            P(("farcp", "nearcp"), None, "tp", None),
            P(("farcp", "nearcp"), "tp", None),
        ),
        check_vma=False,
    )
```

profile of v0, /device:TPU:28, one launch (start us, length us, event | category | flops | bytes accessed | tf_op | source)
XLA Modules:
  0.0 390.4 jit_solution(15981875329838903006)
XLA Ops:
  0.6 188.6 %all_to_all.21 = bf16[16,512,4,128]{3,2,1,0:T(4,128)(2,1)} all-to-all(bf16[16,512,4,128]{3,2,1,0:T(4,128)(2,1)} %param.3), channel_id=1, replica_groups=mesh['farcp'=4,'nearcp'=4,'tp'=2] {'farcp','nearcp'}, dimensions={0} | all-to-all | bytes 16777216 | tf_op jit(solution)/shard_map/all_to_all | solution.py:23
  189.2 6.7 %all-to-all-start.1 = ((bf16[16,512,4,128]{3,2,1,0:T(4,128)(2,1)}), bf16[16,512,4,128]{3,2,1,0:T(4,128)(2,1)}, u32[]{:S(2)}, u32[]{:S(2)}) async-start(bf16[16,512,4,128]{3,2,1,0:T(4,128)(2,1)} %param.4), calls=%async_computation.1 | async-start | bytes 16777216 | tf_op jit(solution)/shard_map/all_to_all | solution.py:24
  196.0 9.4 %fusion = (f32[8192,64]{0,1:T(8,128)}, f32[8192,64]{0,1:T(8,128)S(1)}) fusion(f32[8192,64]{0,1:T(8,128)} %param.5), kind=kLoop, calls=%fused_computation.6 | loop fusion | bytes 6291456 | tf_op jit(solution)/shard_map/cos | solution.py:9
  205.4 3.8 copy.6
  209.2 2.8 copy.7
  212.0 0.0 copy-start.2
  212.0 0.0 copy-start.3
  212.0 5.9 %bitcast_convert_fusion = f32[1,4096,8,128]{3,2,1,0:T(8,128)S(1)} fusion(bf16[1,4096,8,128]{3,2,1,0:T(8,128)(2,1)} %bitcast.9), kind=kLoop, calls=%fused_computation.5 | loop fusion | flops 4194304 | bytes 25165824 | tf_op jit(solution)/shard_map/convert_element_type | solution.py:17
  217.9 0.0 copy-done.2
  217.9 0.1 copy-done.3
  218.0 14.5 %multiply_subtract_fusion = (f32[1,8192,4,64]{3,2,1,0:T(4,128)}, f32[1,8192,4,64]{3,2,1,0:T(4,128)}) fusion(f32[1,8192,4,128]{3,2,1,0:T(4,128)S(1)} %bitcast.8, f32[8192,64]{1,0:T(8,128)S(1)} %copy-done.3, f32[8192,64]{1,0:T(8,128)S(1)} %copy-done.2), kind=kLoop, calls=%fused_computation.3 | loop fusion | flops 12582912 | bytes 37748736 | tf_op jit(solution)/shard_map/sub | solution.py:12
  232.4 0.0 copy-start
  232.4 0.0 copy-start.1
  232.4 19.4 %abs_reduce_fusion = f32[4,128]{1,0:T(4,128)S(1)} fusion(f32[1,8192,4,64]{3,2,1,0:T(4,128)} %get-tuple-element.4, f32[1,8192,4,64]{3,2,1,0:T(4,128)} %get-tuple-element.3), kind=kLoop, calls=%fused_computation.1 | loop fusion | flops 12582400 | bytes 16779264 | tf_op jit(solution)/shard_map/reduce_max | solution.py:27
  251.8 0.0 copy-done
  251.8 1.0 copy-done.1
  252.8 0.0 copy-start.4
  252.8 10.3 %divide_convert_fusion = bf16[1,8192,4,128]{3,2,1,0:T(4,128)(2,1)} fusion(f32[4,128]{1,0:T(4,128)S(1)} %abs_reduce_fusion, f32[1,8192,4,64]{3,2,1,0:T(4,128)S(1)} %copy-done.1, f32[1,8192,4,64]{3,2,1,0:T(4,128)S(1)} %copy-done), kind=kLoop, calls=%fused_computation.4 | loop fusion | flops 12582912 | bytes 25167872 | tf_op jit(solution)/shard_map/convert_element_type | solution.py:28
  263.0 0.0 copy-done.4
  263.0 119.3 %all-to-all-done.1 = bf16[16,512,4,128]{3,2,1,0:T(4,128)(2,1)} async-done(((bf16[16,512,4,128]{3,2,1,0:T(4,128)(2,1)}), bf16[16,512,4,128]{3,2,1,0:T(4,128)(2,1)}, u32[]{:S(2)}, u32[]{:S(2)}) %all-to-all-start.1) | async-done | bytes 8388640 | tf_op jit(solution)/shard_map/all_to_all | solution.py:24
  382.3 8.1 %copy.9 = bf16[1,8192,4,128]{3,2,1,0:T(4,128)(2,1)} copy(bf16[1,8192,4,128]{3,2,1,0:T(4,128)(2,1)} %bitcast.2) | data formatting | bytes 16777216
Async XLA Ops:
  189.2 193.1 %all-to-all-start.1 = ((bf16[16,512,4,128]{3,2,1,0:T(4,128)(2,1)}), bf16[16,512,4,128]{3,2,1,0:T(4,128)(2,1)}, u32[]{:S(2)}, u32[]{:S(2)}) async-start(bf16[16,512,4,128]{3,2,1,0:T(4,128)(2,1)} %param.4), calls=%async_computation.1 | async-start | bytes 16777216 | tf_op jit(solution)/shard_map/all_to_all | solution.py:24
  212.0 5.9 %copy-start.2 = (f32[8192,64]{1,0:T(8,128)S(1)}, f32[8192,64]{1,0:T(8,128)}, u32[]{:S(2)}) copy-start(f32[8192,64]{1,0:T(8,128)} %copy.6) | copy-start | bytes 6291460
  212.0 6.0 %copy-start.3 = (f32[8192,64]{1,0:T(8,128)S(1)}, f32[8192,64]{1,0:T(8,128)}, u32[]{:S(2)}) copy-start(f32[8192,64]{1,0:T(8,128)} %copy.7) | copy-start | bytes 6291460
  232.4 19.4 %copy-start = (f32[1,8192,4,64]{3,2,1,0:T(4,128)S(1)}, f32[1,8192,4,64]{3,2,1,0:T(4,128)}, u32[]{:S(2)}) copy-start(f32[1,8192,4,64]{3,2,1,0:T(4,128)} %get-tuple-element.3) | copy-start | bytes 25165828
  232.4 20.4 %copy-start.1 = (f32[1,8192,4,64]{3,2,1,0:T(4,128)S(1)}, f32[1,8192,4,64]{3,2,1,0:T(4,128)}, u32[]{:S(2)}) copy-start(f32[1,8192,4,64]{3,2,1,0:T(4,128)} %get-tuple-element.4) | copy-start | bytes 25165828
  252.8 10.3 %copy-start.4 = (f32[4,128]{1,0:T(4,128)}, f32[4,128]{1,0:T(4,128)S(1)}, u32[]{:S(2)}) copy-start(f32[4,128]{1,0:T(4,128)S(1)} %abs_reduce_fusion) | copy-start | bytes 6148
where the time goes:
time: 391 us; the launch traced here: 390 us
  blocking collectives  189 us (48%)
  waiting for transfers between devices  119 us (30%)
  other arithmetic  50 us (13%)
  local copies, waits for them, and re-layouts  25.1 us (6%)
  starting transfers between devices  6.73 us (2%)
    all_to_all x1, blocking collectives, body(): lax.all_to_all(raw_keys, ('farcp', 'nearcp'), split_axis=0, concat_axis=1...  189 us
    all_to_all x1, waiting for transfers between devices, body(): lax.all_to_all(raw_values, ('farcp', 'nearcp'), split_axis=0, concat_axis...  119 us
    reduce_max x1, other arithmetic, body(): key_scale = jnp.max(jnp.abs(turned_keys), axis=1)  19.4 us
    sub x1, other arithmetic, turn_pairs(): first * cosine - second * sine  14.5 us
    cos x2, local copies, waits for them, and re-layouts, turn_pairs(): jnp.cos(angle)[None, :, None, :]  13.3 us
    convert_element_type x1, other arithmetic, body(): narrow_keys = (turned_keys / key_scale[:, None]).astype(jnp.bfloat16)  10.3 us
    unnamed x11, local copies, waits for them, and re-layouts  9.08 us
  transfers between devices with their start and end apart: 1, of which 1 were waited for; matrix products, arithmetic and copies ran while one was open for 17% of the time, Pallas kernels for 0%

commit v1 on v0

--- a/solution.py
+++ b/solution.py
@@ -2,6 +2,13 @@
 import jax.numpy as jnp
 from jax import lax
 from jax.sharding import PartitionSpec as P
+
+
+def swap_blocks(block, axis, split, join):
+    size = lax.axis_size(axis)
+    blocks = jnp.stack(jnp.split(block, size, axis=split), axis=0)
+    blocks = lax.all_to_all(blocks, axis, split_axis=0, concat_axis=0)
+    return jnp.concatenate(blocks, axis=join)
 
 
 def turn_pairs(vectors, angle):
@@ -20,7 +27,7 @@
 
 def body(raw_keys, raw_values, turn_angle):
     moved_keys, stored_values = (
-        lax.all_to_all(raw_keys, ("farcp", "nearcp"), split_axis=0, concat_axis=1, tiled=True),
+        swap_blocks(raw_keys, ("farcp", "nearcp"), 0, 1),
         lax.all_to_all(raw_values, ("farcp", "nearcp"), split_axis=0, concat_axis=1, tiled=True),
     )
     turned_keys = ready_to_store(moved_keys, turn_angle)

time: 391 us -> 412 us (1.054)
  local copies, waits for them, and re-layouts: 25.1 us -> 45.2 us
    unnamed x11 -> x26, local copies, waits for them, and re-layouts: 9.08 us -> 27.9 us
  transfers between devices with their start and end apart: 1 -> 1, of which waited for: 1 -> 1; matrix products, arithmetic and copies ran while one was open for 17% -> 16% of each run, Pallas kernels for 0% -> 0%
where the time goes in v1:
time: 412 us; the launch traced here: 410 us
  blocking collectives  188 us (46%)
  waiting for transfers between devices  119 us (29%)
  other arithmetic  50.5 us (12%)
  local copies, waits for them, and re-layouts  45.2 us (11%)
  starting transfers between devices  6.73 us (2%)
    all_to_all x1, blocking collectives, swap_blocks(): blocks = lax.all_to_all(blocks, axis, split_axis=0, concat_axis=0)  188 us
    all_to_all x1, waiting for transfers between devices, body(): lax.all_to_all(raw_values, ('farcp', 'nearcp'), split_axis=0, concat_axis...  119 us
    unnamed x26, local copies, waits for them, and re-layouts  27.9 us
    reduce_max x1, other arithmetic, body(): key_scale = jnp.max(jnp.abs(turned_keys), axis=1)  19.4 us
    sub x1, other arithmetic, turn_pairs(): first * cosine - second * sine  14.5 us
    cos x2, local copies, waits for them, and re-layouts, turn_pairs(): jnp.cos(angle)[None, :, None, :]  13.3 us
    convert_element_type x1, other arithmetic, body(): narrow_keys = (turned_keys / key_scale[:, None]).astype(jnp.bfloat16)  10.3 us
  transfers between devices with their start and end apart: 1, of which 1 were waited for; matrix products, arithmetic and copies ran while one was open for 16% of the time, Pallas kernels for 0%

profile of v1, /device:TPU:28, one launch (start us, length us, event | category | flops | bytes accessed | tf_op | source)
XLA Modules:
  0.0 410.3 jit_solution(16739852657971664723)
XLA Ops:
  0.6 1.2 bitcast_dynamic-update-slice_fusion.15
  1.9 1.3 bitcast_dynamic-update-slice_fusion.14
  3.1 1.3 bitcast_dynamic-update-slice_fusion.13
  4.4 1.3 bitcast_dynamic-update-slice_fusion.12
  5.6 1.3 bitcast_dynamic-update-slice_fusion.11
  6.9 1.3 bitcast_dynamic-update-slice_fusion.10
  8.2 1.3 bitcast_dynamic-update-slice_fusion.9
  9.4 1.3 bitcast_dynamic-update-slice_fusion.8
  10.7 1.3 bitcast_dynamic-update-slice_fusion.7
  12.0 1.3 bitcast_dynamic-update-slice_fusion.6
  13.2 1.3 bitcast_dynamic-update-slice_fusion.5
  14.5 1.3 bitcast_dynamic-update-slice_fusion.4
  15.7 1.3 bitcast_dynamic-update-slice_fusion.3
  17.0 1.3 bitcast_dynamic-update-slice_fusion.2
  18.3 1.3 bitcast_dynamic-update-slice_fusion.1
  19.5 1.3 bitcast_dynamic-update-slice_fusion
  20.8 188.4 %all_to_all.17 = bf16[16,1,512,4,128]{4,3,2,1,0:T(4,128)(2,1)} all-to-all(bf16[16,1,512,4,128]{4,3,2,1,0:T(4,128)(2,1)S(1)} %bitcast_dynamic-update-slice_fusion), channel_id=1, replica_groups=mesh['farcp'=4,'nearcp'=4,'tp'=2] {'farcp','nearcp'}, dimensions={0} | all-to-all | bytes 16777216 | tf_op jit(solution)/shard_map/all_to_all | solution.py:10
  209.2 6.7 %all-to-all-start.1 = ((bf16[16,512,4,128]{3,2,1,0:T(4,128)(2,1)}), bf16[16,512,4,128]{3,2,1,0:T(4,128)(2,1)}, u32[]{:S(2)}, u32[]{:S(2)}) async-start(bf16[16,512,4,128]{3,2,1,0:T(4,128)(2,1)} %param.4), calls=%async_computation.1 | async-start | bytes 16777216 | tf_op jit(solution)/shard_map/all_to_all | solution.py:31
  215.9 9.4 %fusion = (f32[8192,64]{0,1:T(8,128)}, f32[8192,64]{0,1:T(8,128)S(1)}) fusion(f32[8192,64]{0,1:T(8,128)} %param.5), kind=kLoop, calls=%fused_computation.21 | loop fusion | bytes 6291456 | tf_op jit(solution)/shard_map/cos | solution.py:16
  225.3 3.8 copy.6
  229.2 2.8 copy.7
  231.9 0.0 copy-start.2
  231.9 0.0 copy-start.3
  231.9 6.4 %convert.1 = f32[1,8192,4,128]{3,2,1,0:T(4,128)S(1)} convert(bf16[1,8192,4,128]{3,2,1,0:T(4,128)(2,1)} %bitcast.36) | non-fusion elementwise | flops 4194304 | bytes 25165824 | tf_op jit(solution)/shard_map/convert_element_type | solution.py:24
  238.3 0.0 copy-done.2
  238.3 0.0 copy-done.3
  238.4 14.5 %multiply_subtract_fusion = (f32[1,8192,4,64]{3,2,1,0:T(4,128)}, f32[1,8192,4,64]{3,2,1,0:T(4,128)}) fusion(f32[1,8192,4,128]{3,2,1,0:T(4,128)S(1)} %convert.1, f32[8192,64]{1,0:T(8,128)S(1)} %copy-done.3, f32[8192,64]{1,0:T(8,128)S(1)} %copy-done.2), kind=kLoop, calls=%fused_computation.3 | loop fusion | flops 12582912 | bytes 37748736 | tf_op jit(solution)/shard_map/sub | solution.py:19
  252.8 0.0 copy-start
  252.8 0.0 copy-start.1
  252.8 19.4 %abs_reduce_fusion = f32[4,128]{1,0:T(4,128)S(1)} fusion(f32[1,8192,4,64]{3,2,1,0:T(4,128)} %get-tuple-element.4, f32[1,8192,4,64]{3,2,1,0:T(4,128)} %get-tuple-element.3), kind=kLoop, calls=%fused_computation.1 | loop fusion | flops 12582400 | bytes 16779264 | tf_op jit(solution)/shard_map/reduce_max | solution.py:34
  272.2 0.0 copy-done
  272.2 1.0 copy-done.1
  273.2 0.0 copy-start.4
  273.2 10.3 %divide_convert_fusion = bf16[1,8192,4,128]{3,2,1,0:T(4,128)(2,1)} fusion(f32[4,128]{1,0:T(4,128)S(1)} %abs_reduce_fusion, f32[1,8192,4,64]{3,2,1,0:T(4,128)S(1)} %copy-done.1, f32[1,8192,4,64]{3,2,1,0:T(4,128)S(1)} %copy-done), kind=kLoop, calls=%fused_computation.4 | loop fusion | flops 12582912 | bytes 25167872 | tf_op jit(solution)/shard_map/convert_element_type | solution.py:35
  283.5 0.0 copy-done.4
  283.5 118.8 %all-to-all-done.1 = bf16[16,512,4,128]{3,2,1,0:T(4,128)(2,1)} async-done(((bf16[16,512,4,128]{3,2,1,0:T(4,128)(2,1)}), bf16[16,512,4,128]{3,2,1,0:T(4,128)(2,1)}, u32[]{:S(2)}, u32[]{:S(2)}) %all-to-all-start.1) | async-done | bytes 8388640 | tf_op jit(solution)/shard_map/all_to_all | solution.py:31
  402.3 8.1 %copy.24 = bf16[1,8192,4,128]{3,2,1,0:T(4,128)(2,1)} copy(bf16[1,8192,4,128]{3,2,1,0:T(4,128)(2,1)} %bitcast.18) | data formatting | bytes 16777216
Async XLA Ops:
  209.2 193.1 %all-to-all-start.1 = ((bf16[16,512,4,128]{3,2,1,0:T(4,128)(2,1)}), bf16[16,512,4,128]{3,2,1,0:T(4,128)(2,1)}, u32[]{:S(2)}, u32[]{:S(2)}) async-start(bf16[16,512,4,128]{3,2,1,0:T(4,128)(2,1)} %param.4), calls=%async_computation.1 | async-start | bytes 16777216 | tf_op jit(solution)/shard_map/all_to_all | solution.py:31
  231.9 6.4 %copy-start.2 = (f32[8192,64]{1,0:T(8,128)S(1)}, f32[8192,64]{1,0:T(8,128)}, u32[]{:S(2)}) copy-start(f32[8192,64]{1,0:T(8,128)} %copy.6) | copy-start | bytes 6291460
  231.9 6.4 %copy-start.3 = (f32[8192,64]{1,0:T(8,128)S(1)}, f32[8192,64]{1,0:T(8,128)}, u32[]{:S(2)}) copy-start(f32[8192,64]{1,0:T(8,128)} %copy.7) | copy-start | bytes 6291460
  252.8 19.4 %copy-start = (f32[1,8192,4,64]{3,2,1,0:T(4,128)S(1)}, f32[1,8192,4,64]{3,2,1,0:T(4,128)}, u32[]{:S(2)}) copy-start(f32[1,8192,4,64]{3,2,1,0:T(4,128)} %get-tuple-element.3) | copy-start | bytes 25165828
  252.8 20.4 %copy-start.1 = (f32[1,8192,4,64]{3,2,1,0:T(4,128)S(1)}, f32[1,8192,4,64]{3,2,1,0:T(4,128)}, u32[]{:S(2)}) copy-start(f32[1,8192,4,64]{3,2,1,0:T(4,128)} %get-tuple-element.4) | copy-start | bytes 25165828
  273.2 10.3 %copy-start.4 = (f32[4,128]{1,0:T(4,128)}, f32[4,128]{1,0:T(4,128)S(1)}, u32[]{:S(2)}) copy-start(f32[4,128]{1,0:T(4,128)S(1)} %abs_reduce_fusion) | copy-start | bytes 6148
